TPU v7x, 128 devices: a whole 4x4x4 slice. The times are simulated.
128 devices in a mesh: ctx: 16 (over x, y), head: 8 (over z, core).
Axes of the slice: x: 4, y: 4, z: 4, core: 2. Of those that a mesh axis runs over, the one named last changes fastest.
Arguments:
- query_low: bfloat16 [2, 1536], P(None, 'ctx'), may hold values from -6 to 6
- query_weight: bfloat16 [1536, 73728], P('ctx', 'head'), may hold values from -0.21875 to 0.21875
- latent_cache: bfloat16 [2, 131072, 576], P(None, ('ctx', 'head')), may hold values from -300 to 300
- lengths: int32 [2], replicated, may hold values from 81921 to 131072
- value_weight: bfloat16 [128, 512, 128], P('head'), may hold values from -2 to 2
- output_weight: bfloat16 [16384, 7168], P('head', 'ctx'), may hold values from -0.0625 to 0.0625
Outputs:
- attended: bfloat16 [2, 7168], P(None, ('ctx', 'head'))
All inputs are finite; a program needn't handle non-finite values.
Results may differ from a plain program's by a relative error of at most 0.028.
Values may be sent and summed in bfloat16 or wider, within the bound.
No kernel may reach another device: no remote copies, remote signals or barrier semaphores. Data moves between devices by JAX's collectives and lax.ppermute only.
A program may use at most 192 MiB of HBM per device.

v0:
```python
import jax
import jax.numpy as jnp
from jax import lax
from jax.sharding import Mesh
from jax.sharding import PartitionSpec as P

KV_RANK = 512
CTX = ("ctx_0", "ctx_1")
HEAD = ("head_0", "head_1")
CTX_HEAD = ("ctx_0", "ctx_1", "head_0", "head_1")


softmax_scale = 0.07216878


def sent_to_all(x, axis):
    copies = jnp.broadcast_to(x, (lax.axis_size(axis), *x.shape))
    return lax.all_to_all(copies, axis, split_axis=0, concat_axis=0, tiled=True)


def over_copies(x, axis):
    return sent_to_all(x, axis).sum(axis=0)


def in_order(parts, dim):
    parts = jnp.moveaxis(parts, 0, dim)
    lengths = parts.shape
    return parts.reshape(*lengths[:dim], lengths[dim] * lengths[dim + 1], *lengths[dim + 2 :])


def gathered_copies(x, axis, dim):
    return in_order(sent_to_all(x, axis), dim)


def over_copies_2(x, axis):
    return sent_to_all(x, axis).max(axis=0)


def over_axes(x, axes):
    far, near = axes
    nearer = over_copies_2(x, near)
    return over_copies_2(nearer, far)


def in_blocks(x, dim, count):
    before, after = (x.shape[:dim], x.shape[dim + 1 :])
    return jnp.moveaxis(x.reshape(*before, count, -1, *after), dim, 0)


def summed_on_arrival(x, axis, dim):
    count = lax.axis_size(axis)
    parts = lax.all_to_all(in_blocks(x, dim, count), axis, 0, 0, tiled=True)
    return jnp.sum(parts, axis=0)


def sum_in_two_steps(x, axes, dim):
    far, near = axes
    own = summed_on_arrival(in_blocks(x, dim, lax.axis_size(far)), near, dim + 1)
    return jnp.sum(lax.all_to_all(own, far, 0, 0, tiled=True), axis=0)


def side_by_side(arrays, axis, dim, along):
    columns = [a.reshape(*a.shape[:along], -1) for a in arrays]
    both = jnp.concatenate(columns, axis=along)
    filled, at, gathered = (sum_in_two_steps(both, axis, dim), 0, [])
    for a, column in zip(arrays, columns):
        share = filled[..., at : at + column.shape[along]]
        gathered.append(share.reshape(*share.shape[:along], *a.shape[along:]))
        at += column.shape[along]
    return tuple(gathered)


def turned_gather(arrays, axis, dims):
    turned = [jnp.moveaxis(a, dim, 0) for a, dim in zip(arrays, dims)]
    both = jnp.concatenate([t.reshape(len(t), -1) for t in turned], axis=1)
    filled, at, gathered = (lax.all_gather(both, axis, axis=0, tiled=True), 0, [])
    for t, dim in zip(turned, dims):
        share = filled[:, at : at + t[0].size].reshape(-1, *t.shape[1:])
        gathered.append(jnp.moveaxis(share, 0, dim))
        at += t[0].size
    return tuple(gathered)


def on_device(query_low, query_weight, latent_cache, lengths, value_weight, output_weight):
    ctx_count = lax.axis_size(CTX)
    head_count = lax.axis_size(HEAD)
    sequences = query_low.shape[0]
    local_heads = value_weight.shape[0]
    all_heads = local_heads * head_count
    per_share = local_heads // ctx_count
    width = latent_cache.shape[2]
    partial_value = jnp.dot(query_low, query_weight, preferred_element_type=jnp.float32)
    summed = over_copies(partial_value, CTX).astype(jnp.bfloat16)
    gathered = gathered_copies(summed, HEAD, 1)
    queries = gathered.reshape(sequences, all_heads, width)
    span = latent_cache.shape[1]
    offset = (lax.axis_index(CTX) * head_count + lax.axis_index(HEAD)) * span
    places = offset + jnp.arange(span, dtype=jnp.int32)
    usable = (places[None, :] < lengths[:, None])[:, None, :]
    scores = (
        jnp.einsum("bhc,bpc->bhp", queries, latent_cache, preferred_element_type=jnp.float32)
        * softmax_scale
    )
    scores = jnp.where(usable, scores, -1e30)
    local_max = jnp.max(scores, axis=2)
    probabilities = jnp.where(usable, jnp.exp(scores - local_max[..., None]), 0.0)
    totals = jnp.sum(probabilities, axis=2)
    numerators = jnp.einsum(
        "bhp,bpc->bhc",
        probabilities.astype(jnp.bfloat16),
        latent_cache[:, :, :KV_RANK],
        preferred_element_type=jnp.float32,
    )
    highest = over_axes(local_max, (("ctx_0", "ctx_1", "head_0"), "head_1"))
    factor = jnp.exp(local_max - highest)

    def regroup(values):
        dims_now = values.shape
        grouped = values.reshape((sequences, head_count, ctx_count, per_share) + dims_now[2:])
        return jnp.swapaxes(grouped, 1, 2).reshape(dims_now)

    share_totals, share_numerators = side_by_side(
        (regroup(totals * factor), regroup(numerators * factor[..., None])),
        (("ctx_0", "ctx_1", "head_0"), "head_1"),
        1,
        2,
    )
    head_totals, head_numerators = turned_gather((share_totals, share_numerators), CTX, (1, 1))
    latent_out = (head_numerators / head_totals[..., None]).astype(jnp.bfloat16)
    values = jnp.einsum(
        "bhc,hcv->bhv", latent_out, value_weight, preferred_element_type=jnp.float32
    ).astype(jnp.bfloat16)
    projected = jnp.dot(
        values.reshape(sequences, -1), output_weight, preferred_element_type=jnp.float32
    )
    return summed_on_arrival(projected, HEAD, 1).astype(jnp.bfloat16)


def solution(mesh):
    finer = Mesh(mesh.devices.reshape(4, 4, 4, 2), ("ctx_0", "ctx_1", "head_0", "head_1"))
    return jax.shard_map(
        on_device,
        mesh=finer,
        in_specs=(
            P(None, CTX),
            P(CTX, HEAD),
            P(None, CTX_HEAD, None),
            P(),
            P(HEAD, None, None),
            P(HEAD, CTX),
        ),
        out_specs=P(None, CTX_HEAD),
        check_vma=False,
    )
```

profile of v0, /device:TPU:1, one launch (start us, length us, event | category | flops | bytes accessed | tf_op | source)
XLA Modules:
  0.0 125.0 jit_solution(3201359506912485582)
XLA Ops:
  0.0 2.0 %fusion.23 = f32[2,9216]{1,0:T(2,128)S(1)} fusion(bf16[2,96]{1,0:T(2,128)(2,1)} %param.6, bf16[96,9216]{1,0:T(8,128)(2,1)} %param.7), kind=kOutput, calls=%fused_computation.30 | convolution fusion | flops 3538944 | bytes 1843584 | tf_op jit(solution)/shard_map/dot_general | solution.py:92
  2.0 1.3 %broadcast_in_dim.37 = f32[16,2,9216]{2,1,0:T(2,128)} broadcast(f32[2,9216]{1,0:T(2,128)S(1)} %fusion.23), dimensions={1,2} | broadcast | bytes 1253376 | tf_op jit(solution)/shard_map/broadcast_in_dim | solution.py:17
  3.3 7.7 %all-to-all-start = ((f32[16,2,9216]{2,1,0:T(2,128)}), f32[16,2,9216]{2,1,0:T(2,128)S(1)}, u32[]{:S(2)}, u32[]{:S(2)}) async-start(f32[16,2,9216]{2,1,0:T(2,128)} %broadcast_in_dim.37), calls=%async_computation | async-start | bytes 2359296 | tf_op jit(solution)/shard_map/all_to_all | solution.py:18
  11.0 17.0 %all-to-all-done = f32[16,2,9216]{2,1,0:T(2,128)S(1)} async-done(((f32[16,2,9216]{2,1,0:T(2,128)}), f32[16,2,9216]{2,1,0:T(2,128)S(1)}, u32[]{:S(2)}, u32[]{:S(2)}) %all-to-all-start) | async-done | bytes 1179680 | tf_op jit(solution)/shard_map/all_to_all | solution.py:18
  28.0 0.4 reduce_sum.49
  28.4 0.9 broadcast_in_dim.38
  29.3 8.6 %all-to-all-start.1 = ((bf16[8,2,9216]{2,1,0:T(2,128)(2,1)}), bf16[8,2,9216]{2,1,0:T(2,128)(2,1)S(1)}, u32[]{:S(2)}, u32[]{:S(2)}) async-start(bf16[8,2,9216]{2,1,0:T(2,128)(2,1)} %broadcast_in_dim.38), calls=%async_computation.1 | async-start | bytes 589824 | tf_op jit(solution)/shard_map/all_to_all | solution.py:18
  37.9 6.7 %all-to-all-done.1 = bf16[8,2,9216]{2,1,0:T(2,128)(2,1)S(1)} async-done(((bf16[8,2,9216]{2,1,0:T(2,128)(2,1)}), bf16[8,2,9216]{2,1,0:T(2,128)(2,1)S(1)}, u32[]{:S(2)}, u32[]{:S(2)}) %all-to-all-start.1) | async-done | bytes 294944 | tf_op jit(solution)/shard_map/all_to_all | solution.py:18
  45.0 2.4 %fusion.22 = (f32[2,128]{1,0:T(2,128)S(1)}, f32[2,128,1024]{2,1,0:T(8,128)S(1)}) fusion(bf16[2,128,576]{2,1,0:T(8,128)(2,1)S(1)} %reshape_reshape.4, bf16[2,1024,576]{1,2,0:T(8,128)(2,1)} %param.8, pred[2,1024]{1,0:T(4,128)(4,1)S(1)} %broadcast_compare_fusion), kind=kOutput, calls=%fused_computation.29 | convolution fusion | flops 302776064 | bytes 3705856 | tf_op jit(solution)/shard_map/bhc,bpc->bhp/dot_general | solution.py:101
  47.4 4.4 %all_to_all.35 = f32[2,2,128]{2,1,0:T(2,128)S(1)} all-to-all(f32[2,2,128]{2,1,0:T(2,128)S(1)} %broadcast_in_dim.41), channel_id=1, replica_groups=mesh['ctx_0'=4,'ctx_1'=4,'head_0'=4,'head_1'=2] {'head_1'}, dimensions={0} | all-to-all | bytes 4096 | tf_op jit(solution)/shard_map/all_to_all | solution.py:18
  51.8 0.6 broadcast_in_dim.42
  52.5 4.6 %all-to-all-start.3 = ((f32[64,2,128]{2,1,0:T(2,128)}), f32[64,2,128]{2,1,0:T(2,128)S(1)}, u32[]{:S(2)}, u32[]{:S(2)}) async-start(f32[64,2,128]{2,1,0:T(2,128)} %broadcast_in_dim.42), calls=%async_computation.3 | async-start | bytes 131072 | tf_op jit(solution)/shard_map/all_to_all | solution.py:18
  57.1 0.3 fusion.10
  57.4 8.1 %all-to-all-done.3 = f32[64,2,128]{2,1,0:T(2,128)S(1)} async-done(((f32[64,2,128]{2,1,0:T(2,128)}), f32[64,2,128]{2,1,0:T(2,128)S(1)}, u32[]{:S(2)}, u32[]{:S(2)}) %all-to-all-start.3) | async-done | bytes 65568 | tf_op jit(solution)/shard_map/all_to_all | solution.py:18
  65.6 2.4 %fusion.3 = f32[2,128,512]{2,1,0:T(8,128)S(1)} fusion(bf16[2,1024,576]{1,2,0:T(8,128)(2,1)} %param.8, f32[2,128,1024]{2,1,0:T(8,128)S(1)} %get-tuple-element.8, f32[2,128]{1,0:T(2,128)S(1)} %get-tuple-element.7, pred[2,1024]{1,0:T(4,128)(4,1)S(1)} %broadcast_compare_fusion, f32[2,128]{1,0:T(2,128)S(1)} %get-tuple-element.6), kind=kOutput, calls=%fused_computation.4 | convolution fusion | flops 269352960 | bytes 3674112 | tf_op jit(solution)/shard_map/bhp,bpc->bhc/dot_general | solution.py:108
  68.1 0.4 copy.37
  68.8 0.7 maximum_bitcast_fusion
  69.7 5.6 %all_to_all.36 = f32[2,64,2,1,513]{4,2,1,3,0:T(2,128)S(1)} all-to-all(f32[2,64,2,1,513]{4,2,1,3,0:T(2,128)S(1)} %copy.39), channel_id=1, replica_groups=mesh['ctx_0'=4,'ctx_1'=4,'head_0'=4,'head_1'=2] {'head_1'}, dimensions={0} | all-to-all | bytes 1050624 | tf_op jit(solution)/shard_map/all_to_all | solution.py:52
  75.3 0.6 reduce_sum.51
  75.9 14.7 %all_to_all.37 = f32[64,2,1,513]{3,1,2,0:T(2,128)S(1)} all-to-all(f32[64,2,1,513]{3,1,2,0:T(2,128)S(1)} %bitcast.59), channel_id=1, replica_groups=mesh['ctx_0'=4,'ctx_1'=4,'head_0'=4,'head_1'=2] {'ctx_0','ctx_1','head_0'}, dimensions={0} | all-to-all | bytes 525312 | tf_op jit(solution)/shard_map/all_to_all | solution.py:59
  91.0 16.2 %all-gather = f32[16,1,1026]{2,1,0:T(1,128)S(1)} all-gather(f32[1,1,1026]{2,1,0:T(1,128)S(1)} %maximum_bitcast_fusion.1), channel_id=1, replica_groups=mesh['ctx_0'=4,'ctx_1'=4,'head_0'=4,'head_1'=2] {'ctx_0','ctx_1'}, dimensions={0}, use_global_device_ids=true | all-gather | bytes 69768 | tf_op jit(solution)/shard_map/all_gather | solution.py:76
  107.4 2.7 %fusion.8 = f32[8,2,56]{2,1,0:T(2,128)S(1)} fusion(bf16[8,56,2048]{2,1,0:T(8,128)(2,1)} %bitcast.58, bf16[16,512,128]{2,1,0:T(8,128)(2,1)S(1)} %copy-done, f32[16,2,512]{2,1,0:T(2,128)S(1)} %reshape.93, f32[2,16]{0,1:T(8,128)S(1)} %slice_bitcast_fusion), kind=kOutput, calls=%fused_computation.8 | convolution fusion | flops 7901184 | bytes 4001408 | tf_op jit(solution)/shard_map/dot_general | solution.py:133
  110.1 14.3 %all_to_all.38 = f32[8,2,56]{2,1,0:T(2,128)S(1)} all-to-all(f32[8,2,56]{2,1,0:T(2,128)S(1)} %fusion.8), channel_id=1, replica_groups=mesh['ctx_0'=4,'ctx_1'=4,'head_0'=4,'head_1'=2] {'head_0','head_1'}, dimensions={0} | all-to-all | bytes 7168 | tf_op jit(solution)/shard_map/all_to_all | solution.py:52
  124.5 0.5 reduce_sum.55
  (25 shorter events, 1.5 us)
Async XLA Ops:
  0.0 107.4 %copy-start = (bf16[16,512,128]{2,1,0:T(8,128)(2,1)S(1)}, bf16[16,512,128]{2,1,0:T(8,128)(2,1)}, u32[]{:S(2)}) copy-start(bf16[16,512,128]{2,1,0:T(8,128)(2,1)} %param.10) | copy-start | bytes 6291460
  3.3 34.6 %copy-start.1 = (s32[2]{0:T(128)S(1)}, s32[2]{0:T(128)}, u32[]{:S(2)}) copy-start(s32[2]{0:T(128)} %param.9) | copy-start | bytes 28
  3.3 24.7 %all-to-all-start = ((f32[16,2,9216]{2,1,0:T(2,128)}), f32[16,2,9216]{2,1,0:T(2,128)S(1)}, u32[]{:S(2)}, u32[]{:S(2)}) async-start(f32[16,2,9216]{2,1,0:T(2,128)} %broadcast_in_dim.37), calls=%async_computation | async-start | bytes 2359296 | tf_op jit(solution)/shard_map/all_to_all | solution.py:18
  29.3 15.3 %all-to-all-start.1 = ((bf16[8,2,9216]{2,1,0:T(2,128)(2,1)}), bf16[8,2,9216]{2,1,0:T(2,128)(2,1)S(1)}, u32[]{:S(2)}, u32[]{:S(2)}) async-start(bf16[8,2,9216]{2,1,0:T(2,128)(2,1)} %broadcast_in_dim.38), calls=%async_computation.1 | async-start | bytes 589824 | tf_op jit(solution)/shard_map/all_to_all | solution.py:18
  52.5 13.1 %all-to-all-start.3 = ((f32[64,2,128]{2,1,0:T(2,128)}), f32[64,2,128]{2,1,0:T(2,128)S(1)}, u32[]{:S(2)}, u32[]{:S(2)}) async-start(f32[64,2,128]{2,1,0:T(2,128)} %broadcast_in_dim.42), calls=%async_computation.3 | async-start | bytes 131072 | tf_op jit(solution)/shard_map/all_to_all | solution.py:18
where the time goes:
time: 126 us; the launch traced here: 125 us
  blocking collectives  55.4 us (44%)
  waiting for transfers between devices  31.8 us (25%)
  starting transfers between devices  20.9 us (17%)
  matrix products  9.5 us (8%)
  local copies, waits for them, and re-layouts  4.34 us (3%)
  other arithmetic  2.99 us (2%)
    all_to_all x3, waiting for transfers between devices, sent_to_all(): return lax.all_to_all(copies, axis, split_axis=0, concat_axis=0, tiled=True)  31.8 us
    all_to_all x3, starting transfers between devices, sent_to_all(): return lax.all_to_all(copies, axis, split_axis=0, concat_axis=0, tiled=True)  20.9 us
    all_to_all x2, blocking collectives, summed_on_arrival(): parts = lax.all_to_all(in_blocks(x, dim, count), axis, 0, 0, tiled=True)  20 us
    all_gather x1, blocking collectives, turned_gather(): lax.all_gather(both, axis, axis=0, tiled=True)  16.2 us
    all_to_all x1, blocking collectives, sum_in_two_steps(): return jnp.sum(lax.all_to_all(own, far, 0, 0, tiled=True), axis=0)  14.7 us
    all_to_all x1, blocking collectives, sent_to_all(): return lax.all_to_all(copies, axis, split_axis=0, concat_axis=0, tiled=True)  4.44 us
    broadcast_in_dim x4, local copies, waits for them, and re-layouts, sent_to_all(): copies = jnp.broadcast_to(x, (lax.axis_size(axis), *x.shape))  2.82 us
    dot_general x1, matrix products, on_device(): jnp.dot(values.reshape(sequences, -1), output_weight, preferred_element_t...  2.71 us
  transfers between devices with their start and end apart: 3, of which 3 were waited for; matrix products, arithmetic and copies ran while one was open for 0% of the time, Pallas kernels for 0%

commit v1 on v0

v1 whole, which is shorter than its diff:
```python
import jax
import jax.numpy as jnp
from jax import lax
from jax.sharding import Mesh
from jax.sharding import PartitionSpec as P

KV_RANK = 512
CTX = ("ctx_0", "ctx_1")
HEAD = ("head_0", "head_1")
CTX_HEAD = CTX + HEAD
HEAD_CTX = HEAD + CTX
SCALE = 0.07216878
LANES = 128


def exchange(x, axes):
    return lax.all_to_all(x, axes, 0, 0, tiled=True)


def to_all(x, axes):
    return exchange(jnp.broadcast_to(x, (lax.axis_size(axes), *x.shape)), axes)


def three_terms(x):
    high = lax.reduce_precision(x, 8, 7)
    rest = x - high
    middle = lax.reduce_precision(rest, 8, 7)
    low = rest - middle
    return [term.astype(jnp.bfloat16) for term in (high, middle, low)]


def packed(vectors, top, total):
    seqs, heads, _ = vectors.shape
    rows = jnp.swapaxes(vectors, 0, 1).reshape(heads, -1).astype(jnp.bfloat16)
    terms = jnp.concatenate(three_terms(top) + three_terms(total), axis=0).T
    terms = jnp.pad(terms, ((0, 0), (0, LANES - terms.shape[1])))
    return jnp.concatenate([rows, terms], axis=1)


def combined(parts, seqs):
    peers, heads, width = parts.shape
    terms = parts[:, :, width - LANES :].astype(jnp.float32)
    terms = terms[:, :, : 6 * seqs].reshape(peers, heads, 2, 3, seqs).sum(axis=3)
    tops, totals = terms[:, :, 0], terms[:, :, 1]
    top = jnp.max(tops, axis=0)
    factor = jnp.exp(tops - top)
    total = jnp.sum(totals * factor, axis=0)
    vectors = parts[:, :, : width - LANES].reshape(peers, heads, seqs, -1)
    summed = jnp.sum(vectors.astype(jnp.float32) * factor[..., None], axis=0)
    return summed, top, total


def on_device(query_low, query_weight, latent_cache, lengths, value_weight, output_weight):
    ctx_count = lax.axis_size(CTX)
    head_count = lax.axis_size(HEAD)
    seqs = query_low.shape[0]
    local_heads = value_weight.shape[0]
    width = latent_cache.shape[2]
    span = latent_cache.shape[1]

    partial = jnp.dot(query_low, query_weight, preferred_element_type=jnp.float32)
    partial = jnp.swapaxes(partial.reshape(seqs, ctx_count, -1), 0, 1)
    own = exchange(partial, CTX).sum(axis=0).astype(jnp.bfloat16)
    queries = to_all(own, HEAD_CTX).reshape(local_heads * head_count, seqs, width)

    offset = (lax.axis_index(CTX) * head_count + lax.axis_index(HEAD)) * span
    places = offset + jnp.arange(span, dtype=jnp.int32)
    usable = (places[None, :] < lengths[:, None])[:, None, :]
    scores = jnp.einsum(
        "hbc,bpc->bhp", queries, latent_cache, preferred_element_type=jnp.float32
    )
    scores = jnp.where(usable, scores * SCALE, -1e30)
    top = jnp.max(scores, axis=2)
    weights = jnp.where(usable, jnp.exp(scores - top[..., None]), 0.0)
    total = jnp.sum(weights, axis=2)
    numerators = jnp.einsum(
        "bhp,bpc->bhc",
        weights.astype(jnp.bfloat16),
        latent_cache[:, :, :KV_RANK],
        preferred_element_type=jnp.float32,
    )
    sent = packed(numerators, top, total).reshape(head_count, local_heads, -1)
    numerators, top, total = combined(exchange(sent, HEAD), seqs)
    values = jnp.einsum(
        "hbc,hcv->bhv",
        numerators.astype(jnp.bfloat16),
        value_weight,
        preferred_element_type=jnp.float32,
    )
    values, _, total = combined(to_all(packed(values, top.T, total.T), CTX), seqs)
    values = (values / total[..., None]).astype(jnp.bfloat16)
    values = jnp.swapaxes(values, 0, 1).reshape(seqs, -1)
    projected = jnp.dot(values, output_weight, preferred_element_type=jnp.float32)
    projected = jnp.swapaxes(projected.reshape(seqs, head_count, -1), 0, 1)
    return exchange(projected, HEAD).sum(axis=0).astype(jnp.bfloat16)


def solution(mesh):
    finer = Mesh(mesh.devices.reshape(4, 4, 4, 2), CTX_HEAD)
    return jax.shard_map(
        on_device,
        mesh=finer,
        in_specs=(
            P(None, CTX),
            P(CTX, HEAD),
            P(None, CTX_HEAD, None),
            P(),
            P(HEAD, None, None),
            P(HEAD, CTX),
        ),
        out_specs=P(None, CTX_HEAD),
        check_vma=False,
    )
```

time: 126 us -> 78.2 us (0.62)
  blocking collectives: 55.4 us -> 29.6 us
  waiting for transfers between devices: 31.8 us -> 17.9 us
  starting transfers between devices: 20.9 us -> 16.1 us
  other arithmetic: 2.99 us -> 1.29 us
  matrix products: 9.5 us -> 8.14 us
    all_gather x1 -> x0, blocking collectives: 16.2 us -> none  [turned_gather(): lax.all_gather(both, axis, axis=0, tiled=True)]
    all_to_all x3 -> x2, waiting for transfers between devices: 31.8 us -> 17.9 us  [exchange(): return lax.all_to_all(x, axes, 0, 0, tiled=True)]
    all_to_all x4 -> x3, blocking collectives: 39.1 us -> 29.6 us  [exchange(): return lax.all_to_all(x, axes, 0, 0, tiled=True)]
    all_to_all x3 -> x2, starting transfers between devices: 20.9 us -> 16.1 us  [exchange(): return lax.all_to_all(x, axes, 0, 0, tiled=True)]
    broadcast_in_dim x4 -> x2, local copies, waits for them, and re-layouts: 2.82 us -> 0.91 us  [to_all(): return exchange(jnp.broadcast_to(x, (lax.axis_size(axes), *x.shape)), axes)]
    dot_general x3 -> x4, matrix products: 7.52 us -> 6.15 us  [the longest x1 2.52 us: on_device(): jnp.einsum('hbc,bpc->bhp', queries, latent_cache, preferred_element_type=...]
  transfers between devices with their start and end apart: 3 -> 2, of which waited for: 3 -> 2; matrix products, arithmetic and copies ran while one was open for 0% -> 0% of each run, Pallas kernels for 0% -> 0%
where the time goes in v1:
time: 78.2 us; the launch traced here: 77.9 us
  blocking collectives  29.6 us (38%)
  waiting for transfers between devices  17.9 us (23%)
  starting transfers between devices  16.1 us (21%)
  matrix products  8.14 us (10%)
  local copies, waits for them, and re-layouts  4.67 us (6%)
  other arithmetic  1.29 us (2%)
    all_to_all x3, blocking collectives, exchange(): return lax.all_to_all(x, axes, 0, 0, tiled=True)  29.6 us
    all_to_all x2, waiting for transfers between devices, exchange(): return lax.all_to_all(x, axes, 0, 0, tiled=True)  17.9 us
    all_to_all x2, starting transfers between devices, exchange(): return lax.all_to_all(x, axes, 0, 0, tiled=True)  16.1 us
    dot_general x1, matrix products, on_device(): jnp.einsum('hbc,bpc->bhp', queries, latent_cache, preferred_element_type=...  2.52 us
    dot_general x1, matrix products, on_device(): jnp.dot(values, output_weight, preferred_element_type=jnp.float32)  2.41 us
    dot_general x1, matrix products, on_device(): jnp.dot(query_low, query_weight, preferred_element_type=jnp.float32)  1.99 us
  transfers between devices with their start and end apart: 2, of which 2 were waited for; matrix products, arithmetic and copies ran while one was open for 0% of the time, Pallas kernels for 0%

profile of v1, /device:TPU:1, one launch (start us, length us, event | category | flops | bytes accessed | tf_op | source)
XLA Modules:
  0.0 77.9 jit_solution(10081888315569675689)
XLA Ops:
  0.0 2.0 %fusion.37 = f32[2,9216]{1,0:T(2,128)S(1)} fusion(bf16[2,96]{1,0:T(2,128)(2,1)} %param.6, bf16[96,9216]{1,0:T(8,128)(2,1)} %param.7), kind=kOutput, calls=%fused_computation.66 | convolution fusion | flops 3538944 | bytes 1843584 | tf_op jit(solution)/shard_map/dot_general | solution.py:61
  2.1 0.7 copy.85
  2.8 7.6 %all-to-all-start = ((f32[16,2,576]{2,1,0:T(2,128)}), f32[16,2,576]{2,1,0:T(2,128)S(1)}, u32[]{:S(2)}, u32[]{:S(2)}) async-start(f32[16,2,576]{2,1,0:T(2,128)} %bitcast.77), calls=%async_computation | async-start | bytes 163840 | tf_op jit(solution)/shard_map/all_to_all | solution.py:17
  10.4 6.6 %all-to-all-done = f32[16,2,576]{2,1,0:T(2,128)S(1)} async-done(((f32[16,2,576]{2,1,0:T(2,128)}), f32[16,2,576]{2,1,0:T(2,128)S(1)}, u32[]{:S(2)}, u32[]{:S(2)}) %all-to-all-start) | async-done | bytes 73760 | tf_op jit(solution)/shard_map/all_to_all | solution.py:17
  17.0 0.9 %broadcast_in_dim.34 = bf16[128,2,576]{2,1,0:T(2,128)(2,1)} broadcast(bf16[2,576]{1,0:T(2,128)(2,1)S(1)} %reduce_sum.85), dimensions={1,2} | broadcast | bytes 297216 | tf_op jit(solution)/shard_map/broadcast_in_dim | solution.py:21
  17.9 8.5 %all-to-all-start.1 = ((bf16[128,2,576]{2,1,0:T(2,128)(2,1)}), bf16[128,2,576]{2,1,0:T(2,128)(2,1)S(1)}, u32[]{:S(2)}, u32[]{:S(2)}) async-start(bf16[128,2,576]{2,1,0:T(2,128)(2,1)} %broadcast_in_dim.34), calls=%async_computation.1 | async-start | bytes 655360 | tf_op jit(solution)/shard_map/all_to_all | solution.py:17
  26.5 11.3 %all-to-all-done.1 = bf16[128,2,576]{2,1,0:T(2,128)(2,1)S(1)} async-done(((bf16[128,2,576]{2,1,0:T(2,128)(2,1)}), bf16[128,2,576]{2,1,0:T(2,128)(2,1)S(1)}, u32[]{:S(2)}, u32[]{:S(2)}) %all-to-all-start.1) | async-done | bytes 294944 | tf_op jit(solution)/shard_map/all_to_all | solution.py:17
  37.8 2.5 %fusion.36 = (f32[2,128]{1,0:T(2,128)S(1)}, f32[2,128,1024]{2,1,0:T(8,128)S(1)}) fusion(bf16[2,1024,576]{1,2,0:T(8,128)(2,1)} %param.8, bf16[128,2,576]{2,1,0:T(2,128)(2,1)S(1)} %all-to-all-done.1, pred[2,1024]{1,0:T(4,128)(4,1)S(1)} %broadcast_compare_fusion), kind=kOutput, calls=%fused_computation.65 | convolution fusion | flops 302776064 | bytes 3705856 | tf_op jit(solution)/shard_map/hbc,bpc->bhp/dot_general | solution.py:69
  40.3 0.3 fusion.9
  40.7 0.8 %fusion.6 = bf16[128,2,512]{2,0,1:T(8,128)(2,1)S(1)} fusion(bf16[2,1024,576]{1,2,0:T(8,128)(2,1)S(1)} %copy-done.1, f32[2,128,1024]{2,1,0:T(8,128)S(1)} %get-tuple-element.22, f32[2,128]{1,0:T(2,128)S(1)} %get-tuple-element.21, pred[2,1024]{1,0:T(4,128)(4,1)S(1)} %broadcast_compare_fusion), kind=kOutput, calls=%fused_computation.5 | convolution fusion | flops 269352960 | bytes 3412992 | tf_op jit(solution)/shard_map/bhp,bpc->bhc/dot_general | solution.py:76
  41.5 0.2 copy.59
  41.8 0.2 copy.60
  42.0 10.8 %all_to_all.25 = bf16[8,16,1152]{2,1,0:T(8,128)(2,1)S(1)} all-to-all(bf16[8,16,1152]{2,1,0:T(8,128)(2,1)S(1)} %bitcast.80), channel_id=1, replica_groups=mesh['ctx_0'=4,'ctx_1'=4,'head_0'=4,'head_1'=2] {'head_0','head_1'}, dimensions={0} | all-to-all | bytes 589824 | tf_op jit(solution)/shard_map/all_to_all | solution.py:17
  53.4 0.2 mul.52
  53.6 0.5 mul.53
  54.4 0.4 convolution_convert_fusion
  54.9 9.9 %all_to_all.26 = bf16[16,16,384]{2,1,0:T(8,128)(2,1)S(1)} all-to-all(bf16[16,16,384]{2,1,0:T(8,128)(2,1)S(1)} %broadcast_in_dim.37), channel_id=1, replica_groups=mesh['ctx_0'=4,'ctx_1'=4,'head_0'=4,'head_1'=2] {'ctx_0','ctx_1'}, dimensions={0} | all-to-all | bytes 393216 | tf_op jit(solution)/shard_map/all_to_all | solution.py:17
  64.8 0.2 copy.76
  65.2 0.2 copy.67
  65.3 0.3 mul.56
  65.7 0.2 mul.57
  66.1 2.4 %convolution_bitcast_fusion = f32[8,2,56]{2,1,0:T(2,128)S(1)} fusion(bf16[8,56,2048]{2,1,0:T(8,128)(2,1)} %bitcast.79, f32[16,2,128]{2,1,0:T(2,128)S(1)} %copy.71, f32[2,16]{0,1:T(8,128)S(1)} %copy.70), kind=kOutput, calls=%fused_computation.7 | convolution fusion | flops 3678208 | bytes 1855104 | tf_op jit(solution)/shard_map/dot_general | solution.py:93
  68.5 8.8 %all_to_all.27 = f32[8,2,56]{2,1,0:T(2,128)S(1)} all-to-all(f32[8,2,56]{2,1,0:T(2,128)S(1)} %convolution_bitcast_fusion), channel_id=1, replica_groups=mesh['ctx_0'=4,'ctx_1'=4,'head_0'=4,'head_1'=2] {'head_0','head_1'}, dimensions={0} | all-to-all | bytes 7168 | tf_op jit(solution)/shard_map/all_to_all | solution.py:17
  77.3 0.5 reduce_sum.95
  (37 shorter events, 1.6 us)
Async XLA Ops:
  0.0 54.4 %copy-start = (bf16[16,512,128]{2,1,0:T(8,128)(2,1)S(1)}, bf16[16,512,128]{2,1,0:T(8,128)(2,1)}, u32[]{:S(2)}) copy-start(bf16[16,512,128]{2,1,0:T(8,128)(2,1)} %param.10) | copy-start | bytes 6291460
  0.0 26.4 %copy-start.2 = (s32[2]{0:T(128)S(1)}, s32[2]{0:T(128)}, u32[]{:S(2)}) copy-start(s32[2]{0:T(128)} %param.9) | copy-start | bytes 28
  2.8 14.2 %all-to-all-start = ((f32[16,2,576]{2,1,0:T(2,128)}), f32[16,2,576]{2,1,0:T(2,128)S(1)}, u32[]{:S(2)}, u32[]{:S(2)}) async-start(f32[16,2,576]{2,1,0:T(2,128)} %bitcast.77), calls=%async_computation | async-start | bytes 163840 | tf_op jit(solution)/shard_map/all_to_all | solution.py:17
  17.9 19.9 %all-to-all-start.1 = ((bf16[128,2,576]{2,1,0:T(2,128)(2,1)}), bf16[128,2,576]{2,1,0:T(2,128)(2,1)S(1)}, u32[]{:S(2)}, u32[]{:S(2)}) async-start(bf16[128,2,576]{2,1,0:T(2,128)(2,1)} %broadcast_in_dim.34), calls=%async_computation.1 | async-start | bytes 655360 | tf_op jit(solution)/shard_map/all_to_all | solution.py:17
  37.8 2.9 %copy-start.1 = (bf16[2,1024,576]{1,2,0:T(8,128)(2,1)S(1)}, bf16[2,1024,576]{1,2,0:T(8,128)(2,1)}, u32[]{:S(2)}) copy-start(bf16[2,1024,576]{1,2,0:T(8,128)(2,1)} %param.8) | copy-start | bytes 7077892

commit v2 on v1

v2 whole, which is shorter than its diff:
```python
import functools

import jax
import jax.numpy as jnp
from jax import lax
from jax.experimental import pallas as pl
from jax.experimental.pallas import tpu as pltpu
from jax.sharding import Mesh
from jax.sharding import PartitionSpec as P

KV_RANK = 512
CTX = ("ctx_0", "ctx_1")
HEAD = ("head_0", "head_1")
CTX_HEAD = CTX + HEAD
GATHER = ("head_0", "ctx_0")
SCALE = 0.07216878
MASKED = -1e30
FLOOR = -1e29
LANES = 128
LAST = (((1,), (1,)), ((), ()))
F32 = jnp.float32
BF16 = jnp.bfloat16

VMEM = pl.BlockSpec(memory_space=pltpu.VMEM)
SMEM = pl.BlockSpec(memory_space=pltpu.SMEM)
HBM = pl.BlockSpec(memory_space=pltpu.HBM)


def exchange(x, axes):
    return lax.all_to_all(x, axes, 0, 0, tiled=True)


def three_terms(x):
    high = x.astype(BF16).astype(F32)
    rest = x - high
    middle = rest.astype(BF16).astype(F32)
    return high, middle, rest - middle


def terms_tile(top, total):
    rows, seqs = top.shape
    lane = lax.broadcasted_iota(jnp.int32, (rows, LANES), 1)
    tile = jnp.zeros((rows, LANES), F32)
    at = 0
    for part in three_terms(top) + three_terms(total):
        for b in range(seqs):
            tile = jnp.where(lane == at, part[:, b : b + 1], tile)
            at += 1
    return tile.astype(BF16)


def from_terms(tile, seqs):
    tile = tile.astype(F32)
    part = [tile[:, k * seqs : (k + 1) * seqs] for k in range(6)]
    return part[0] + part[1] + part[2], part[3] + part[4] + part[5]


def rescaled(tiles, seqs):
    pairs = [from_terms(tile, seqs) for tile in tiles]
    top = functools.reduce(jnp.maximum, [t for t, _ in pairs])
    factors = [jnp.exp(t - top) for t, _ in pairs]
    total = sum(n * f for (_, n), f in zip(pairs, factors))
    return top, total, factors


def project_queries(chunks, copies, low_ref, weight_ref, out_ref, held, sems):
    width = held.shape[2]
    loads = [
        pltpu.make_async_copy(
            weight_ref.at[:, pl.ds(k * width, width)], held.at[k], sems.at[k]
        )
        for k in range(chunks)
    ]
    for load in loads:
        load.start()
    low = low_ref[...]
    for k in range(chunks):
        loads[k].wait()
        part = jnp.dot(low, held[k], preferred_element_type=F32)
        for n in range(copies):
            out_ref[k * copies + n] = part


def sum_queries(parts_ref, out_ref, rows):
    peers, seqs, _ = parts_ref.shape
    width = out_ref.shape[2]
    heads = out_ref.shape[1] // seqs
    total = parts_ref[0]
    for k in range(1, peers):
        total = total + parts_ref[k]
    for b in range(seqs):
        for j in range(heads):
            rows[b * heads + j : b * heads + j + 1, :] = total[
                b : b + 1, j * width : (j + 1) * width
            ]
    done = rows[...].astype(BF16)
    for k in range(out_ref.shape[0]):
        out_ref[k] = done


def attend(lengths_ref, query_ref, own_ref, other_ref, out_ref, rows):
    groups, both, width = query_ref.shape
    seqs, _, span = own_ref.shape
    each = both // seqs
    heads = groups * each
    core = lax.axis_index("head_1")
    pair = (
        lax.axis_index(CTX) * lax.axis_size("head_0") + lax.axis_index("head_0")
    ) * lax.axis_size("head_1")
    starts = ((pair + core) * span, (pair + 1 - core) * span)
    for g in range(groups):
        for b in range(seqs):
            rows[b, g * each : (g + 1) * each, :] = query_ref[
                g, b * each : (b + 1) * each, :
            ].astype(F32)
    tops, totals = [], []
    place = lax.broadcasted_iota(jnp.int32, (heads, span), 1)
    share = out_ref.shape[1]
    for b in range(seqs):
        query = rows[b].astype(BF16)
        scores = []
        for start, block in zip(starts, (own_ref, other_ref)):
            raw = jnp.dot(query, block[b], preferred_element_type=F32)
            scores.append(jnp.where(place < lengths_ref[b] - start, raw * SCALE, MASKED))
        top = jnp.maximum(
            jnp.max(scores[0], axis=1, keepdims=True),
            jnp.max(scores[1], axis=1, keepdims=True),
        )
        top = jnp.maximum(top, FLOOR)
        weights = [jnp.exp(s - top) for s in scores]
        total = jnp.sum(weights[0], axis=1, keepdims=True) + jnp.sum(
            weights[1], axis=1, keepdims=True
        )
        numerator = sum(
            lax.dot_general(w.astype(BF16), block[b, :KV_RANK, :], LAST, preferred_element_type=F32)
            for w, block in zip(weights, (own_ref, other_ref))
        ).astype(BF16)
        for k in range(out_ref.shape[0]):
            out_ref[k, :, b * KV_RANK : (b + 1) * KV_RANK] = numerator[
                k * share : (k + 1) * share
            ]
        tops.append(top)
        totals.append(total)
    lane = lax.broadcasted_iota(jnp.int32, (heads, LANES), 1)
    top = jnp.where(lane == 0, tops[0], tops[1])[:, :seqs]
    total = jnp.where(lane == 0, totals[0], totals[1])[:, :seqs]
    tile = terms_tile(top, total)
    for k in range(out_ref.shape[0]):
        out_ref[k, :, seqs * KV_RANK :] = tile[k * share : (k + 1) * share]


def project_values(parts_ref, weight_ref, out_ref):
    peers, heads, width = parts_ref.shape
    seqs = (width - LANES) // KV_RANK
    top, total, factors = rescaled(
        [parts_ref[k, :, width - LANES :] for k in range(peers)], seqs
    )
    halves = []
    for b in range(seqs):
        halves.append(
            sum(
                parts_ref[k, :, b * KV_RANK : (b + 1) * KV_RANK].astype(F32)
                * factors[k][:, b : b + 1]
                for k in range(peers)
            )
        )
    stacked = jnp.concatenate(halves, axis=0).astype(BF16)
    row = lax.broadcasted_iota(jnp.int32, (seqs * heads, LANES), 0)
    values = jnp.zeros((seqs * heads, LANES), F32)
    for h in range(heads):
        one = jnp.dot(stacked, weight_ref[h], preferred_element_type=F32)
        values = jnp.where(lax.rem(row, heads) == h, one, values)
    values = values.astype(BF16)
    tile = terms_tile(top, total)
    for k in range(out_ref.shape[0]):
        out_ref[k, : seqs * heads, :] = values
        out_ref[k, seqs * heads :, :] = tile


def project_output(parts_ref, weight_ref, out_ref, flat):
    peers, rows, lanes = parts_ref.shape
    seqs = out_ref.shape[1]
    heads = rows // (seqs + 1)
    _, total, factors = rescaled(
        [parts_ref[k, seqs * heads :, :] for k in range(peers)], seqs
    )
    for b in range(seqs):
        values = sum(
            parts_ref[k, b * heads : (b + 1) * heads, :].astype(F32) * factors[k][:, b : b + 1]
            for k in range(peers)
        )
        values = values / total[:, b : b + 1]
        for h in range(heads):
            flat[b : b + 1, h * lanes : (h + 1) * lanes] = values[h : h + 1]
    result = lax.dot_general(
        flat[...].astype(BF16), weight_ref[...], LAST, preferred_element_type=F32
    )
    width = out_ref.shape[2]
    for k in range(out_ref.shape[0]):
        out_ref[k] = result[:, k * width : (k + 1) * width]


def call(body, name, out_shape, out_dtype, in_specs, scratch=(), limit=8):
    return pl.pallas_call(
        body,
        name=name,
        out_shape=jax.ShapeDtypeStruct(out_shape, out_dtype),
        in_specs=in_specs,
        out_specs=VMEM,
        scratch_shapes=list(scratch),
        compiler_params=pltpu.CompilerParams(vmem_limit_bytes=limit * 2**20),
    )


def on_device(query_low, query_weight, latent_cache, lengths, value_weight, output_weight):
    ctx_count = lax.axis_size(CTX)
    head_count = lax.axis_size(HEAD)
    chunks = lax.axis_size("ctx_0")
    depth_count = lax.axis_size("head_0")
    seqs, depth = query_low.shape
    local_heads = value_weight.shape[0]
    width = latent_cache.shape[2]
    columns = query_weight.shape[1]
    each = local_heads // chunks

    latent_cache = jnp.swapaxes(latent_cache, 1, 2)
    other_cache = lax.ppermute(latent_cache, "head_1", [(0, 1), (1, 0)])

    partial = call(
        functools.partial(project_queries, chunks, ctx_count // chunks),
        "project_queries",
        (ctx_count, seqs, columns // chunks),
        F32,
        [VMEM, HBM],
        [
            pltpu.VMEM((chunks, depth, columns // chunks), BF16),
            pltpu.SemaphoreType.DMA((chunks,)),
        ],
    )(query_low, query_weight)
    partial = exchange(partial, CTX)

    own = call(
        sum_queries,
        "sum_queries",
        (depth_count * chunks, seqs * each, width),
        BF16,
        [VMEM],
        [pltpu.VMEM((seqs * each, width), F32)],
    )(partial)
    queries = exchange(own, GATHER)

    sent = call(
        attend,
        "attend",
        (depth_count, local_heads, seqs * KV_RANK + LANES),
        BF16,
        [SMEM, VMEM, VMEM, VMEM],
        [pltpu.VMEM((seqs, depth_count * local_heads, width), F32)],
        limit=24,
    )(lengths, queries, latent_cache, other_cache)
    arrived = exchange(sent, "head_0")

    values = call(
        project_values,
        "project_values",
        (ctx_count, (seqs + 1) * local_heads, value_weight.shape[2]),
        BF16,
        [VMEM, VMEM],
    )(arrived, value_weight)
    values = exchange(values, CTX)

    projected = call(
        project_output,
        "project_output",
        (head_count, seqs, output_weight.shape[1] // head_count),
        F32,
        [VMEM, VMEM],
        [pltpu.VMEM((seqs, output_weight.shape[0]), F32)],
    )(values, output_weight.T)
    return exchange(projected, HEAD).sum(axis=0).astype(BF16)


def solution(mesh):
    finer = Mesh(mesh.devices.reshape(4, 4, 4, 2), CTX_HEAD)
    return jax.shard_map(
        on_device,
        mesh=finer,
        in_specs=(
            P(None, CTX),
            P(CTX, HEAD),
            P(None, CTX_HEAD, None),
            P(),
            P(HEAD, None, None),
            P(HEAD, CTX),
        ),
        out_specs=P(None, CTX_HEAD),
        check_vma=False,
    )
```

time: 78.2 us -> 67.5 us (0.86)
  blocking collectives: 29.6 us -> 57.5 us
  waiting for transfers between devices: 17.9 us -> 0.01 us
  starting transfers between devices: 16.1 us -> 1.38 us
  matrix products: 8.14 us -> 0 us
  Pallas kernels: 0 us -> 5.58 us
  local copies, waits for them, and re-layouts: 4.67 us -> 2.15 us
    all_to_all x3 -> x5, blocking collectives: 29.6 us -> 57.5 us  [exchange(): return lax.all_to_all(x, axes, 0, 0, tiled=True)]
    all_to_all x2 -> x0, waiting for transfers between devices: 17.9 us -> none  [exchange(): return lax.all_to_all(x, axes, 0, 0, tiled=True)]
    all_to_all x2 -> x0, starting transfers between devices: 16.1 us -> none  [exchange(): return lax.all_to_all(x, axes, 0, 0, tiled=True)]
    dot_general x5 -> x0, matrix products: 8.14 us -> none  [the longest x1 2.52 us: on_device(): jnp.einsum('hbc,bpc->bhp', queries, latent_cache, preferred_element_type=...]
    pallas_call x0 -> x5, Pallas kernels: none -> 5.58 us  [the longest x1 3.15 us: on_device(): call(attend, 'attend', (depth_count, local_heads, seqs * KV_RANK + LANES)...]
    unnamed x12, local copies, waits for them, and re-layouts: 0.7 us -> 2.15 us
    ppermute x0 -> x1, starting transfers between devices: none -> 1.38 us  [on_device(): other_cache = lax.ppermute(latent_cache, 'head_1', [(0, 1), (1, 0)])]
    mul x4 -> x0, local copies, waits for them, and re-layouts: 1.2 us -> none  [combined(): summed = jnp.sum(vectors.astype(jnp.float32) * factor[..., None], axis=0)]
  transfers between devices with their start and end apart: 2 -> 1, of which waited for: 2 -> 0; matrix products, arithmetic and copies ran while one was open for 0% -> 0% of each run, Pallas kernels for 0% -> 2%
where the time goes in v2:
time: 67.5 us; the launch traced here: 67.2 us
  blocking collectives  57.5 us (85%)
  Pallas kernels  5.58 us (8%)
  local copies, waits for them, and re-layouts  2.15 us (3%)
  starting transfers between devices  1.38 us (2%)
    all_to_all x5, blocking collectives, exchange(): return lax.all_to_all(x, axes, 0, 0, tiled=True)  57.5 us
    pallas_call x1, Pallas kernels, on_device(): call(attend, 'attend', (depth_count, local_heads, seqs * KV_RANK + LANES)...  3.15 us
    unnamed x12, local copies, waits for them, and re-layouts  2.15 us
    ppermute x1, starting transfers between devices, on_device(): other_cache = lax.ppermute(latent_cache, 'head_1', [(0, 1), (1, 0)])  1.38 us
  transfers between devices with their start and end apart: 1, of which 0 were waited for; matrix products, arithmetic and copies ran while one was open for 0% of the time, Pallas kernels for 2%

profile of v2, /device:TPU:1, one launch (start us, length us, event | category | flops | bytes accessed | tf_op | source)
XLA Modules:
  0.0 67.2 jit_solution(24581282366397997)
XLA Ops:
  0.0 0.0 copy-start
  0.0 1.4 %collective-permute-start = (bf16[2,576,1024]{2,1,0:T(8,128)(2,1)}, bf16[2,576,1024]{2,1,0:T(8,128)(2,1)S(1)}, u32[]{:S(2)}, u32[]{:S(2)}) collective-permute-start(bf16[2,576,1024]{2,1,0:T(8,128)(2,1)} %bitcast.2), channel_id=1, source_target_pairs={{0,1},{1,0},{2,3},{3,2},{4,5},{5,4},{6,7},{7,6},{8,9},{9,8},{10,11... | collective-permute-start | bytes 7077896 | tf_op jit(solution)/shard_map/ppermute | solution.py:227
  1.4 0.0 copy-start.3
  1.4 1.5 %copy-done.3 = bf16[96,9216]{1,0:T(8,128)(2,1)S(1)} copy-done((bf16[96,9216]{1,0:T(8,128)(2,1)S(1)}, bf16[96,9216]{1,0:T(8,128)(2,1)}, u32[]{:S(2)}) %copy-start.3) | copy-done | bytes 1769496
  2.9 0.0 copy-start.4
  2.9 0.7 copy-done.4
  3.5 0.0 copy-start.5
  3.5 0.9 %project_queries.1 = f32[16,2,2304]{2,1,0:T(2,128)S(1)} custom-call(bf16[2,96]{1,0:T(2,128)(2,1)S(1)} %copy-done.4, bf16[96,9216]{1,0:T(8,128)(2,1)S(1)} %copy-done.3), custom_call_target="tpu_custom_call" | custom-call | tf_op jit(solution)/shard_map/project_queries/pallas_call | solution.py:229
  4.4 14.6 %all_to_all.25.parts_ref = f32[16,2,2304]{2,1,0:T(2,128)S(1)} all-to-all(f32[16,2,2304]{2,1,0:T(2,128)S(1)} %project_queries.1), channel_id=1, replica_groups=mesh['ctx_0'=4,'ctx_1'=4,'head_0'=4,'head_1'=2] {'ctx_0','ctx_1'}, dimensions={0} | all-to-all | bytes 589824 | tf_op jit(solution)/shard_map/all_to_all | solution.py:30
  19.1 0.1 sum_queries.1
  19.2 13.0 %all_to_all.26.query_ref = bf16[16,8,576]{2,1,0:T(8,128)(2,1)S(1)} all-to-all(bf16[16,8,576]{2,1,0:T(8,128)(2,1)S(1)} %sum_queries.1), channel_id=1, replica_groups=mesh['ctx_0'=4,'ctx_1'=4,'head_0'=4,'head_1'=2] {'head_0','ctx_0'}, dimensions={0} | all-to-all | bytes 294912 | tf_op jit(solution)/shard_map/all_to_all | solution.py:30
  32.2 0.0 collective-permute-done.other_ref
  32.2 0.0 copy-done
  32.2 0.0 copy-done.5
  32.3 3.2 %attend.1 = bf16[4,16,1152]{2,1,0:T(8,128)(2,1)S(1)} custom-call(s32[2]{0:T(128)S(1)} %copy-done.5, bf16[16,8,576]{2,1,0:T(8,128)(2,1)S(1)} %all_to_all.26.query_ref, bf16[2,576,1024]{2,1,0:T(8,128)(2,1)S(1)} %bitcast.3, bf16[2,576,1024]{2,1,0:T(8,128)(2,1)S(1)} %collective-permute-done.other_ref), custom_call_target="tpu_custom_call" | custom-call | tf_op jit(solution)/shard_map/attend/pallas_call | solution.py:252
  35.4 0.0 copy-start.2
  35.4 7.4 %all_to_all.27.parts_ref = bf16[4,16,1152]{2,1,0:T(8,128)(2,1)S(1)} all-to-all(bf16[4,16,1152]{2,1,0:T(8,128)(2,1)S(1)} %attend.1), channel_id=1, replica_groups=mesh['ctx_0'=4,'ctx_1'=4,'head_0'=4,'head_1'=2] {'head_0'}, dimensions={0} | all-to-all | bytes 294912 | tf_op jit(solution)/shard_map/all_to_all | solution.py:30
  42.8 0.0 copy-done.1
  42.8 0.6 project_values.1
  43.4 10.2 %all_to_all.28.parts_ref = bf16[16,48,128]{2,1,0:T(8,128)(2,1)S(1)} all-to-all(bf16[16,48,128]{2,1,0:T(8,128)(2,1)S(1)} %project_values.1), channel_id=1, replica_groups=mesh['ctx_0'=4,'ctx_1'=4,'head_0'=4,'head_1'=2] {'ctx_0','ctx_1'}, dimensions={0} | all-to-all | bytes 393216 | tf_op jit(solution)/shard_map/all_to_all | solution.py:30
  53.6 0.0 copy-done.2
  53.6 0.8 %project_output.1 = f32[8,2,56]{2,1,0:T(2,128)S(1)} custom-call(bf16[16,48,128]{2,1,0:T(8,128)(2,1)S(1)} %all_to_all.28.parts_ref, bf16[448,2048]{1,0:T(8,128)(2,1)S(1)} %bitcast.4), custom_call_target="tpu_custom_call" | custom-call | tf_op jit(solution)/shard_map/project_output/pallas_call | solution.py:272
  54.4 12.2 %all_to_all.29 = f32[8,2,56]{2,1,0:T(2,128)S(1)} all-to-all(f32[8,2,56]{2,1,0:T(2,128)S(1)} %project_output.1), channel_id=1, replica_groups=mesh['ctx_0'=4,'ctx_1'=4,'head_0'=4,'head_1'=2] {'head_0','head_1'}, dimensions={0} | all-to-all | bytes 7168 | tf_op jit(solution)/shard_map/all_to_all | solution.py:30
  66.7 0.5 reduce_sum.9
  (1 shorter events, 0.0 us)
Async XLA Ops:
  0.0 32.2 %copy-start = (bf16[2,1024,576]{1,2,0:T(8,128)(2,1)S(1)}, bf16[2,1024,576]{1,2,0:T(8,128)(2,1)}, u32[]{:S(2)}) copy-start(bf16[2,1024,576]{1,2,0:T(8,128)(2,1)} %param.8) | copy-start | bytes 7077892
  0.0 32.2 %collective-permute-start = (bf16[2,576,1024]{2,1,0:T(8,128)(2,1)}, bf16[2,576,1024]{2,1,0:T(8,128)(2,1)S(1)}, u32[]{:S(2)}, u32[]{:S(2)}) collective-permute-start(bf16[2,576,1024]{2,1,0:T(8,128)(2,1)} %bitcast.2), channel_id=1, source_target_pairs={{0,1},{1,0},{2,3},{3,2},{4,5},{5,4},{6,7},{7,6},{8,9},{9,8},{10,11... | collective-permute-start | bytes 7077896 | tf_op jit(solution)/shard_map/ppermute | solution.py:227
  1.4 1.5 %copy-start.3 = (bf16[96,9216]{1,0:T(8,128)(2,1)S(1)}, bf16[96,9216]{1,0:T(8,128)(2,1)}, u32[]{:S(2)}) copy-start(bf16[96,9216]{1,0:T(8,128)(2,1)} %weight_ref.2) | copy-start | bytes 5308420
  2.9 0.7 copy-start.4
  3.5 28.7 %copy-start.5 = (s32[2]{0:T(128)S(1)}, s32[2]{0:T(128)}, u32[]{:S(2)}) copy-start(s32[2]{0:T(128)} %lengths_ref.1) | copy-start | bytes 28
  32.2 10.6 %copy-start.1 = (bf16[16,512,128]{2,1,0:T(8,128)(2,1)S(1)}, bf16[16,512,128]{2,1,0:T(8,128)(2,1)}, u32[]{:S(2)}) copy-start(bf16[16,512,128]{2,1,0:T(8,128)(2,1)} %weight_ref.3) | copy-start | bytes 6291460
  35.4 18.2 %copy-start.2 = (bf16[2048,448]{0,1:T(8,128)(2,1)S(1)}, bf16[2048,448]{0,1:T(8,128)(2,1)}, u32[]{:S(2)}) copy-start(bf16[2048,448]{0,1:T(8,128)(2,1)} %param.11) | copy-start | bytes 5505028
